TPU v7x, 32 devices: a whole 2x2x4 slice. The times are simulated.
32 devices in a mesh: ifg: 16 (over z, y, x), slab: 2 (over core).
Axes of the slice: x: 2, y: 2, z: 4, core: 2. Of those that a mesh axis runs over, the one named last changes fastest.
Arguments:
- phase: float32 [2, 1152, 6144], P('slab', 'ifg'), may hold values from -60 to 60
- corrections: int32 [2, 1152, 6144], P('slab', 'ifg'), may hold values from -1 to 1
- closure_loops: int32 [288, 1152], replicated, may hold values from -1 to 1, as said below
- design: int32 [1152, 288], replicated, may hold values from -1 to 1, as said below
Outputs:
- closure_phase: float32 [2, 288, 6144], P('slab', None, 'ifg')
- displacement: float32 [2, 288, 6144], P('slab', None, 'ifg')
- misfit: float32 [2], P('slab')
Inputs may be any that keep to these rules, and one draw needn't show every extreme that they name: Each row of closure_loops holds +1 at two interferograms and -1 at a third; closure_loops times design is zero. Each row of design holds one +1 and one -1 in different columns; every date is named by some row.
All inputs are finite; a program needn't handle non-finite values.
Results may differ from a plain program's by a relative error of at most 0.0003.
Values sent between devices are 32-bit elements; how exact they have to be, the bound alone decides.
A program may use at most 64 MiB of HBM per device.

v0:
```python
import jax
import jax.numpy as jnp
from jax import lax
from jax.sharding import PartitionSpec as P

ridge_weight = 1.0
two_pi = 6.283185307179586
epsilon = 1e-06
highest = lax.Precision.HIGHEST


def local(phase, corrections, closure_loops, design):
    slab_count = lax.axis_size("slab")
    slab_pixels = phase.shape[2]
    loop_rows = closure_loops.astype(jnp.float32)
    date_count = design.shape[1]
    design_float = design.astype(jnp.float32)
    normal = jnp.dot(design_float.T, design_float, precision=highest) + ridge_weight * jnp.eye(
        date_count, dtype=jnp.float32
    )
    factor = jnp.linalg.cholesky(normal)
    normal_inverse = jax.scipy.linalg.cho_solve(
        (factor, True), jnp.eye(date_count, dtype=jnp.float32)
    )
    corrected_rows = phase[0] + two_pi * corrections[0].astype(jnp.float32)
    gathered = lax.all_to_all(corrected_rows, "ifg", split_axis=1, concat_axis=0, tiled=True)
    closure = jnp.dot(loop_rows, gathered, precision=highest)
    projected = jnp.dot(design_float.T, gathered, precision=highest)
    closure, shifts = (closure, jnp.dot(normal_inverse, projected, precision=highest))
    residual = gathered - jnp.dot(design_float, shifts, precision=highest)
    closure, shifts, squares = (
        closure,
        shifts,
        jnp.sum(residual * residual, axis=0, keepdims=True),
    )
    column_sum = jnp.sum(shifts, axis=1)
    square_sum = jnp.sum(squares)
    own_slot = (jnp.arange(slab_count) == lax.axis_index("slab")).astype(jnp.float32)
    frame_total, by_slab = lax.psum((column_sum, own_slot * square_sum), ("ifg", "slab"))
    slab_square = jnp.sum(by_slab * own_slot)
    frame_mean = frame_total / (slab_count * slab_pixels)
    displacement = shifts - frame_mean[:, None]
    misfit = jnp.sqrt(slab_square / (design.shape[0] * slab_pixels) + epsilon)
    return (closure[None], displacement[None], misfit.reshape(1))


def solution(mesh):
    in_specs = (P("slab", "ifg", None), P("slab", "ifg", None), P(), P())
    out_specs = (P("slab", None, "ifg"), P("slab", None, "ifg"), P("slab"))
    return jax.shard_map(local, mesh=mesh, in_specs=in_specs, out_specs=out_specs, check_vma=False)
```

profile of v0, /device:TPU:0, one launch (start us, length us, event | category | flops | bytes accessed | tf_op | source)
XLA Modules:
  0.0 201.1 jit_solution(12344080122575374951)
XLA Ops:
  0.6 2.2 %multiply_add_fusion = f32[1,72,6144]{2,1,0:T(8,128)S(1)} fusion(f32[1,72,6144]{2,1,0:T(8,128)} %param.4, s32[1,72,6144]{2,1,0:T(8,128)} %param.5), kind=kLoop, calls=%fused_computation.5 | loop fusion | flops 1327104 | bytes 5308416 | tf_op jit(solution)/shard_map/add | solution.py:25
  3.2 1.8 copy.21
  4.9 8.5 %all-to-all-start = ((f32[72,16,384]{2,0,1:T(8,128)}), f32[72,16,384]{2,0,1:T(8,128)S(1)}, u32[]{:S(2)}, u32[]{:S(2)}) async-start(f32[72,16,384]{2,0,1:T(8,128)} %copy.21), calls=%async_computation | async-start | bytes 3538944 | tf_op jit(solution)/shard_map/all_to_all | solution.py:26
  14.0 2.4 %fusion.5 = f32[288,288]{1,0:T(8,128)S(1)} fusion(s32[1152,288]{0,1:T(8,128)S(1)} %copy-done), kind=kOutput, calls=%fused_computation.9 | convolution fusion | flops 1146949632 | bytes 1658880 | tf_op jit(solution)/shard_map/dot_general | solution.py:18
  19.2 11.7 %cholesky.78 = f32[128,128]{1,0:T(8,128)S(1)} custom-call(f32[128,128]{1,0:T(8,128)S(1)} %cholesky.198), custom_call_target="Cholesky" | custom-call | tf_op jit(solution)/shard_map/jit(cholesky)/cholesky | solution.py:21
  31.6 10.4 %custom-call.26 = f32[1,128,128]{1,2,0:T(8,128)} custom-call(f32[1,128,128]{2,1,0:T(8,128)S(1)} %get-tuple-element.27), custom_call_target="InvertDiagBlocksLowerTriangular" | custom-call | tf_op jit(solution)/shard_map/jit(cholesky)/cholesky | solution.py:21
  44.0 1.2 convolution_subtract_fusion.3
  46.4 13.3 %cholesky.164 = f32[128,128]{1,0:T(8,128)} custom-call(f32[128,128]{1,0:T(8,128)} %cholesky.202), custom_call_target="Cholesky" | custom-call | tf_op jit(solution)/shard_map/jit(cholesky)/cholesky | solution.py:21
  59.7 2.0 select_reduce_fusion
  61.7 11.3 %custom-call.27 = f32[1,128,128]{1,2,0:T(8,128)} custom-call(f32[1,128,128]{2,1,0:T(8,128)} %get-tuple-element.24), custom_call_target="InvertDiagBlocksLowerTriangular" | custom-call | tf_op jit(solution)/shard_map/jit(cholesky)/cholesky | solution.py:21
  74.0 1.5 convolution_subtract_fusion.5
  75.5 4.2 %cholesky.186 = f32[32,32]{1,0:T(8,128)} custom-call(f32[32,32]{1,0:T(8,128)} %convolution_subtract_fusion.5), custom_call_target="Cholesky" | custom-call | tf_op jit(solution)/shard_map/jit(cholesky)/cholesky | solution.py:21
  81.2 1.3 compare_reduce_fusion.1
  86.9 5.2 %while.1 = (s32[]{:T(128)}, f32[288,288]{1,0:T(8,128)S(1)}, s32[2,2]{1,0:T(2,128)S(1)}, f32[2,128,128]{2,1,0:T(8,128)}, s32[]{:T(128)}) while((s32[]{:T(128)}, f32[288,288]{1,0:T(8,128)S(1)}, s32[2,2]{1,0:T(2,128)S(1)}, f32[2,128,128]{2,1,0:T(8,128)}, s32[]{:T(128)}) %tuple.30), condition=%wide.while_cond, body=%wide.while_body.sunk | while | flops 2 | bytes 132705 | solution.py:22
  87.5 2.0 bitcast_dynamic-update-slice_fusion.2
  90.1 2.0 bitcast_dynamic-update-slice_fusion.2
  92.1 1.8 pad_maximum_fusion
  93.9 30.9 %custom-call.28 = f32[3,128,128]{1,2,0:T(8,128)} custom-call(f32[3,128,128]{2,1,0:T(8,128)} %pad_maximum_fusion), custom_call_target="InvertDiagBlocksLowerTriangular" | custom-call | tf_op jit(solution)/shard_map/jit(_cho_solve)/triangular_solve | solution.py:22
  124.9 1.2 fusion.29
  126.1 1.2 convolution_subtract_fusion
  127.3 1.3 fusion.42
  130.7 1.5 fusion.47
  133.1 1.3 convolution_subtract_fusion.2
  134.4 1.1 fusion.41
  135.6 1.3 convolution_subtract_fusion.1
  136.9 1.8 fusion.40
  138.7 3.3 %fusion.3 = f32[384,288]{0,1:T(8,128)} fusion(f32[1152,384]{1,0:T(8,128)S(1)} %bitcast.75, s32[1152,288]{0,1:T(8,128)S(1)} %copy-done), kind=kOutput, calls=%fused_computation.7 | convolution fusion | flops 1529155584 | bytes 3538944 | tf_op jit(solution)/shard_map/dot_general | solution.py:28
  142.0 1.9 copy.26
  143.9 2.5 %fusion.54 = (f32[288]{0:T(512)S(1)}, f32[288,384]{1,0:T(8,128)S(1)}) fusion(f32[384,288]{0,1:T(8,128)} %fusion.3, f32[32,288]{0,1:T(8,128)} %copy-done.3, f32[128,288]{0,1:T(8,128)} %copy-done.4, f32[128,288]{0,1:T(8,128)} %fusion.40), kind=kOutput, calls=%fused_computation.93 | convolution fusion | flops 382482144 | bytes 1217664 | tf_op jit(solution)/shard_map/dot_general | solution.py:29
  146.5 5.5 %fusion.12 = f32[]{:T(128)} fusion(f32[1152,384]{0,1:T(8,128)} %copy.26, f32[288,384]{1,0:T(8,128)S(1)} %get-tuple-element.33, s32[1152,288]{0,1:T(8,128)S(1)} %copy-done), kind=kOutput, calls=%fused_computation.21 | convolution fusion | flops 1530482688 | bytes 3538948 | tf_op jit(solution)/shard_map/dot_general | solution.py:30
  152.6 40.6 %all-reduce.3 = (f32[288]{0:T(512)S(1)}, f32[2]{0:T(128)S(1)}) all-reduce(f32[288]{0:T(512)S(1)} %get-tuple-element.32, f32[2]{0:T(128)S(1)} %compare_select_fusion.1), channel_id=1, replica_groups=mesh['ifg'=16,'slab'=2] {'ifg','slab'}, use_global_device_ids=true, to_apply=%region_7.8 | all-reduce | flops 290 | bytes 2320 | tf_op jit(solution)/shard_map/psum | solution.py:39
  195.4 4.6 %fusion.9 = f32[1,288,384]{2,1,0:T(8,128)} fusion(f32[1152,384]{1,0:T(8,128)S(1)} %bitcast.77, s32[288,1152]{1,0:T(8,128)} %param.6), kind=kOutput, calls=%fused_computation.13 | convolution fusion | flops 1529155584 | bytes 3538944 | tf_op jit(solution)/shard_map/dot_general | solution.py:27
  (49 shorter events, 18.9 us)
Async XLA Ops:
  4.9 9.1 %copy-start = (s32[1152,288]{0,1:T(8,128)S(1)}, s32[1152,288]{0,1:T(8,128)}, u32[]{:S(2)}) copy-start(s32[1152,288]{0,1:T(8,128)} %param.7) | copy-start | bytes 3981316
  4.9 133.8 %all-to-all-start = ((f32[72,16,384]{2,0,1:T(8,128)}), f32[72,16,384]{2,0,1:T(8,128)S(1)}, u32[]{:S(2)}, u32[]{:S(2)}) async-start(f32[72,16,384]{2,0,1:T(8,128)} %copy.21), calls=%async_computation | async-start | bytes 3538944 | tf_op jit(solution)/shard_map/all_to_all | solution.py:26
  18.5 0.8 copy-start.5
  30.9 0.6 copy-start.7
  45.2 0.6 copy-start.6
  80.5 3.9 %copy-start.2 = (f32[288,288]{1,0:T(8,128)}, f32[288,288]{1,0:T(8,128)S(1)}, u32[]{:S(2)}) copy-start(f32[288,288]{1,0:T(8,128)S(1)} %get-tuple-element.29) | copy-start | bytes 995332
  92.1 32.7 %copy-start.1 = (f32[288,288]{1,0:T(8,128)}, f32[288,288]{1,0:T(8,128)S(1)}, u32[]{:S(2)}) copy-start(f32[288,288]{1,0:T(8,128)S(1)} %get-tuple-element.83) | copy-start | bytes 995332
  133.1 8.9 %copy-start.3 = (f32[32,288]{0,1:T(8,128)}, f32[32,288]{0,1:T(8,128)S(1)}, u32[]{:S(2)}) copy-start(f32[32,288]{0,1:T(8,128)S(1)} %copy.24) | copy-start | bytes 110596
  135.6 6.5 %copy-start.4 = (f32[128,288]{0,1:T(8,128)}, f32[128,288]{0,1:T(8,128)S(1)}, u32[]{:S(2)}) copy-start(f32[128,288]{0,1:T(8,128)S(1)} %fusion.41) | copy-start | bytes 442372
where the time goes:
time: 203 us; the launch traced here: 201 us
  other arithmetic  96.3 us (47%)
  blocking collectives  40.6 us (20%)
  matrix products  35.9 us (18%)
  local copies, waits for them, and re-layouts  15.3 us (8%)
  starting transfers between devices  8.47 us (4%)
  between operations  4.6 us (2%)
    another operation x10, other arithmetic, local(): factor = jnp.linalg.cholesky(normal)  55.7 us
    psum x1, blocking collectives, local(): lax.psum((column_sum, own_slot * square_sum), ('ifg', 'slab'))  40.6 us
    another operation x7, other arithmetic, local(): jax.scipy.linalg.cho_solve((factor, True), jnp.eye(date_count, dtype=jnp....  35.1 us
    another operation x10, matrix products, local(): jax.scipy.linalg.cho_solve((factor, True), jnp.eye(date_count, dtype=jnp....  12.8 us
    all_to_all x1, starting transfers between devices, local(): lax.all_to_all(corrected_rows, 'ifg', split_axis=1, concat_axis=0, tiled=...  8.47 us
    dot_general x1, matrix products, local(): residual = gathered - jnp.dot(design_float, shifts, precision=highest)  5.48 us
    another operation x6, local copies, waits for them, and re-layouts  5.2 us
    another operation x4, matrix products, local(): factor = jnp.linalg.cholesky(normal)  4.77 us
  transfers between devices with their start and end apart: 1, of which 0 were waited for; matrix products, arithmetic and copies ran while one was open for 60% of the time, Pallas kernels for 0%

commit v1 on v0

v1 whole, which is shorter than its diff:
```python
import functools

import jax
import jax.numpy as jnp
from jax import lax
from jax.experimental import pallas as pl
from jax.experimental.pallas import tpu as pltpu
from jax.sharding import PartitionSpec as P

ridge_weight = 1.0
two_pi = 6.283185307179586
epsilon = 1e-06
highest = lax.Precision.HIGHEST
f32 = jnp.float32
bf16 = jnp.bfloat16
MESH = pl.DeviceIdType.MESH
newton_steps = 2


def dot(a, b):
    return jnp.dot(a, b, preferred_element_type=f32)


def split(a):
    high = a.astype(bf16)
    return high, (a - high.astype(f32)).astype(bf16)


def split_three(a):
    high = a.astype(bf16)
    rest = a - high.astype(f32)
    middle = rest.astype(bf16)
    return high, middle, (rest - middle.astype(f32)).astype(bf16)


def dot_split(a, b):
    a_high, a_low = split(a)
    b_high, b_low = split(b)
    return dot(a_high, b_high) + (dot(a_high, b_low) + dot(a_low, b_high))


def partner(me, k, n):
    if n & (n - 1):
        return lax.rem(me + k, n)
    out, bit = 0, 1
    while bit < n:
        out = out + bit * (((me // bit) % 2 + (k // bit) % 2) % 2)
        bit *= 2
    return out


def kernel(n, slabs, widths, doublings, phase, counts, loops, design, closure_out, shifts_out, total_out,
           phase_v, counts_v, sent, *rest):
    chunk_count = len(widths)
    got, rest = rest[:chunk_count], rest[chunk_count:]
    (loops_v, design_v, design_b, left, stack, normal, row, rows_in, flat,
     in_sem, table_sem, own_sem, send_sem, recv_sem, row_send, row_recv) = rest
    me = lax.axis_index("ifg")
    slab = lax.axis_index("slab")
    rows = phase.shape[1]
    dates = design.shape[1]
    columns = sum(widths)
    starts = [sum(widths[:c]) for c in range(chunk_count)]

    loads = [
        pltpu.make_async_copy(phase.at[0], phase_v, in_sem.at[0]),
        pltpu.make_async_copy(counts.at[0], counts_v, in_sem.at[1]),
    ]
    tables = [
        pltpu.make_async_copy(design, design_v, table_sem.at[0]),
        pltpu.make_async_copy(loops, loops_v, table_sem.at[1]),
    ]
    for copy in loads:
        copy.start()

    barrier = pltpu.get_barrier_semaphore()
    for other in range(slabs):
        far_slab = lax.rem(slab + other, slabs)

        @pl.loop(0 if other else 1, n)
        def _(k):
            pl.semaphore_signal(
                barrier, inc=1, device_id={"ifg": partner(me, k, n), "slab": far_slab}, device_id_type=MESH
            )

    for copy in tables:
        copy.start()
    for copy in loads:
        copy.wait()
    sent[...] = phase_v[...] + two_pi * counts_v[...].astype(f32)
    pl.semaphore_wait(barrier, n * slabs - 1)

    for c in range(chunk_count):
        @pl.loop(0, n - 1)
        def _(step):
            to = partner(me, n - 1 - step, n)
            pltpu.make_async_remote_copy(
                src_ref=sent.at[:, pl.ds(pl.multiple_of(to * columns + starts[c], 128), widths[c])],
                dst_ref=got[c].at[me],
                send_sem=send_sem.at[c],
                recv_sem=recv_sem.at[c],
                device_id={"ifg": to},
                device_id_type=MESH,
            ).start()

    own = [
        pltpu.make_async_copy(
            sent.at[:, pl.ds(pl.multiple_of(me * columns + starts[c], 128), widths[c])], got[c].at[me], own_sem.at[c]
        )
        for c in range(chunk_count)
    ]
    for copy in own:
        copy.start()

    eye_bool = lax.broadcasted_iota(jnp.int32, (dates, dates), 0) == lax.broadcasted_iota(
        jnp.int32, (dates, dates), 1
    )
    eye = eye_bool.astype(f32)
    for copy in tables:
        copy.wait()
    loop_count = loops.shape[0]
    left[0:loop_count, :] = loops_v[...].astype(f32).astype(bf16)
    design_b[...] = design_v[...].astype(f32).astype(bf16)
    left[loop_count:, :] = lax.dot_general(
        eye.astype(bf16), design_b[...], (((1,), (1,)), ((), ())), preferred_element_type=f32
    ).astype(bf16)
    matrix = dot(left[loop_count:, :], design_b[...]) + ridge_weight * eye
    normal[...] = matrix
    bound = jnp.max(jnp.sum(jnp.abs(matrix), axis=1, keepdims=True), axis=0, keepdims=True)
    scale = 2.0 / (bound + ridge_weight)
    stack[0:dates, :] = scale * eye
    stack[dates:, :] = eye - scale * matrix

    @pl.loop(0, doublings)
    def _(step):
        both = stack[...]
        product = dot_split(both, both[dates:, :])
        stack[0:dates, :] = both[0:dates, :] + product[0:dates, :]
        stack[dates:, :] = product[dates:, :]

    @pl.loop(0, newton_steps)
    def _(step):
        inverse = stack[0:dates, :]
        error = eye - jnp.dot(normal[...], inverse, precision=highest)
        stack[0:dates, :] = inverse + jnp.dot(inverse, error, precision=highest)

    squares = jnp.zeros((1, 128), f32)
    date_sums = jnp.zeros((8, dates), f32)
    for c in range(chunk_count):
        width = widths[c]
        own[c].wait()
        pltpu.make_async_copy(got[c].at[pl.ds(0, n - 1)], got[c].at[pl.ds(0, n - 1)], recv_sem.at[c]).wait()
        if rows % 8 == 0:
            held = got[c][...].reshape(n * rows, width)
        else:
            for source in range(n):
                flat[source * rows:(source + 1) * rows, 0:width] = got[c][source]
            held = flat[:, 0:width]
        triple = dot(left[...], jnp.concatenate(split_three(held), axis=1))
        summed = triple[:, 0:width] + (triple[:, width:2 * width] + triple[:, 2 * width:])
        closure_out[:, starts[c]:starts[c] + width] = summed[0:loop_count, :]
        shifts = jnp.dot(stack[0:dates, :], summed[loop_count:, :], precision=highest)
        shifts_out[:, starts[c]:starts[c] + width] = shifts
        modelled = dot(design_b[...], jnp.concatenate(split_three(shifts), axis=1))
        residual = held - (modelled[:, 0:width] + (modelled[:, width:2 * width] + modelled[:, 2 * width:]))
        line = jnp.sum(residual * residual, axis=0, keepdims=True)
        for part in range(width // 128):
            squares = squares + line[:, part * 128:(part + 1) * 128]
        date_sums = date_sums + lax.dot_general(
            jnp.ones((8, width), f32), shifts, (((1,), (1,)), ((), ())), precision=highest,
            preferred_element_type=f32,
        )

    padded = row.shape[2] - 128
    row[0, :, 0:dates] = date_sums[0:1, :]
    row[0, :, padded:] = squares
    mine = slab * n + me
    rows_in[mine, :, :] = row[0]
    for other in range(slabs):
        far_slab = lax.rem(slab + other, slabs)

        @pl.loop(0 if other else 1, n)
        def _(k):
            pltpu.make_async_remote_copy(
                src_ref=row.at[0],
                dst_ref=rows_in.at[mine],
                send_sem=row_send,
                recv_sem=row_recv,
                device_id={"ifg": partner(me, k, n), "slab": far_slab},
                device_id_type=MESH,
            ).start()

    for c in range(chunk_count):
        pltpu.make_async_copy(got[c].at[pl.ds(0, n - 1)], got[c].at[pl.ds(0, n - 1)], send_sem.at[c]).wait()
    everyone = rows_in.at[pl.ds(0, n * slabs - 1)]
    pltpu.make_async_copy(everyone, everyone, row_recv).wait()
    pltpu.make_async_copy(everyone, everyone, row_send).wait()
    total_out[:, 0:padded] = jnp.sum(rows_in[:, :, 0:padded], axis=0)
    total_out[:, padded:] = jnp.sum(rows_in[pl.ds(slab * n, n), :, padded:], axis=0)


def local(phase, corrections, closure_loops, design):
    n = lax.axis_size("ifg")
    slabs = lax.axis_size("slab")
    rows, pixels = phase.shape[1:]
    ifgs, dates = design.shape
    loop_count = closure_loops.shape[0]
    columns = pixels // n
    widths = (columns - 128, 128) if columns > 128 else (columns,)
    padded = -(-dates // 128) * 128
    doublings = 1
    while 2 ** doublings < 4 * ifgs:
        doublings += 1
    vmem = pl.BlockSpec(memory_space=pltpu.VMEM)
    anywhere = pl.BlockSpec(memory_space=pl.ANY)
    dma = pltpu.SemaphoreType.DMA
    closure, shifts, total = pl.pallas_call(
        functools.partial(kernel, n, slabs, widths, doublings),
        out_shape=(
            jax.ShapeDtypeStruct((loop_count, columns), f32),
            jax.ShapeDtypeStruct((dates, columns), f32),
            jax.ShapeDtypeStruct((1, padded + 128), f32),
        ),
        in_specs=[anywhere] * 4,
        out_specs=(vmem, vmem, vmem),
        scratch_shapes=[
            pltpu.VMEM((rows, pixels), f32),
            pltpu.VMEM((rows, pixels), jnp.int32),
            pltpu.VMEM((rows, pixels), f32),
            *[pltpu.VMEM((n, rows, width), f32) for width in widths],
            pltpu.VMEM((loop_count, ifgs), jnp.int32),
            pltpu.VMEM((ifgs, dates), jnp.int32),
            pltpu.VMEM((ifgs, dates), bf16),
            pltpu.VMEM((loop_count + dates, ifgs), bf16),
            pltpu.VMEM((2 * dates, dates), f32),
            pltpu.VMEM((dates, dates), f32),
            pltpu.VMEM((1, 1, padded + 128), f32),
            pltpu.VMEM((n * slabs, 1, padded + 128), f32),
            pltpu.VMEM((8 if rows % 8 == 0 else ifgs, max(widths)), f32),
            dma((2,)),
            dma((2,)),
            dma((len(widths),)),
            dma((len(widths),)),
            dma((len(widths),)),
            dma,
            dma,
        ],
        compiler_params=pltpu.CompilerParams(
            collective_id=0, has_side_effects=True, vmem_limit_bytes=48 * 1024 * 1024
        ),
    )(phase, corrections, closure_loops, design)
    frame_mean = total[0, 0:dates] / (slabs * pixels)
    displacement = shifts - frame_mean[:, None]
    misfit = jnp.sqrt(jnp.sum(total[0, padded:]) / (ifgs * pixels) + epsilon)
    return (closure[None], displacement[None], misfit.reshape(1))


def solution(mesh):
    in_specs = (P("slab", "ifg", None), P("slab", "ifg", None), P(), P())
    out_specs = (P("slab", None, "ifg"), P("slab", None, "ifg"), P("slab"))
    return jax.shard_map(local, mesh=mesh, in_specs=in_specs, out_specs=out_specs, check_vma=False)
```

time: 203 us -> 68.6 us (0.34)
  other arithmetic: 96.3 us -> 2.5 us
  Pallas kernels: 0 us -> 57.1 us
  blocking collectives: 40.6 us -> 0 us
  matrix products: 35.9 us -> 0 us
  local copies, waits for them, and re-layouts: 15.3 us -> 6.23 us
  starting transfers between devices: 8.47 us -> 0 us
  between operations: 4.6 us -> 2.49 us
    another operation x17 -> x0, other arithmetic: 90.8 us -> none  [the longest x10 55.7 us: local(): factor = jnp.linalg.cholesky(normal)]
    pallas_call x0 -> x1, Pallas kernels: none -> 57.1 us  [local(): pl.pallas_call(functools.partial(kernel, n, slabs, widths, doublings), ou...]
    psum x1 -> x0, blocking collectives: 40.6 us -> none  [local(): lax.psum((column_sum, own_slot * square_sum), ('ifg', 'slab'))]
    dot_general x5 -> x0, matrix products: 18.3 us -> none  [the longest x1 5.48 us: local(): residual = gathered - jnp.dot(design_float, shifts, precision=highest)]
    another operation x14 -> x0, matrix products: 17.6 us -> none  [the longest x10 12.8 us: local(): jax.scipy.linalg.cho_solve((factor, True), jnp.eye(date_count, dtype=jnp....]
    all_to_all x1 -> x0, starting transfers between devices: 8.47 us -> none  [local(): lax.all_to_all(corrected_rows, 'ifg', split_axis=1, concat_axis=0, tiled=...]
    another operation x12 -> x0, local copies, waits for them, and re-layouts: 8.32 us -> none
    unnamed x17 -> x10, local copies, waits for them, and re-layouts: 2.31 us -> 6.23 us
  transfers between devices with their start and end apart: 1 -> 0, of which waited for: 0 -> 0; matrix products, arithmetic and copies ran while one was open for 60% -> 0% of each run, Pallas kernels for 0% -> 0%
where the time goes in v1:
time: 68.6 us; the launch traced here: 68.4 us
  Pallas kernels  57.1 us (83%)
  local copies, waits for them, and re-layouts  6.23 us (9%)
  other arithmetic  2.5 us (4%)
  between operations  2.49 us (4%)
    pallas_call x1, Pallas kernels, local(): pl.pallas_call(functools.partial(kernel, n, slabs, widths, doublings), ou...  57.1 us
    unnamed x10, local copies, waits for them, and re-layouts  6.23 us
    broadcast_in_dim x1, other arithmetic, local(): return (closure[None], displacement[None], misfit.reshape(1))  1.88 us

profile of v1, /device:TPU:0, one launch (start us, length us, event | category | flops | bytes accessed | tf_op | source)
XLA Modules:
  0.0 68.4 jit_solution(10887641323879431646)
XLA Ops:
  0.6 0.0 copy-start.2
  0.6 0.0 copy-start
  0.7 3.2 %copy.7.design = s32[1152,288]{1,0:T(8,128)} copy(s32[1152,288]{0,1:T(8,128)} %param.7) | data formatting | bytes 2654208 | tf_op args[3]
  3.9 0.0 copy-done.2
  3.9 0.0 copy-done
  3.9 0.0 copy-start.1
  3.9 1.5 %copy-done.1 = s32[1,72,6144]{2,1,0:T(8,128)S(1)} copy-done((s32[1,72,6144]{2,1,0:T(8,128)S(1)}, s32[1,72,6144]{2,1,0:T(8,128)}, u32[]{:S(2)}) %copy-start.1) | copy-done | bytes 1769496
  5.4 57.1 %shard_map.67 = (f32[288,384]{1,0:T(8,128)S(1)}, f32[288,384]{1,0:T(8,128)S(1)}, f32[1,512]{1,0:T(1,128)S(1)}) custom-call(f32[1,72,6144]{2,1,0:T(8,128)S(1)} %copy-done, s32[1,72,6144]{2,1,0:T(8,128)S(1)} %copy-done.1, s32[288,1152]{1,0:T(8,128)S(1)} %copy-done.2, s32[1152,288]{1,0:T(8,128)} %copy.7.design), custom_call_target="tpu_custom_call" | custom-call | tf_op jit(solution)/shard_map/pallas_call | solution.py:217
  62.5 0.0 copy-start.3
  62.5 0.8 %copy-done.3 = f32[288,384]{1,0:T(8,128)} copy-done((f32[288,384]{1,0:T(8,128)}, f32[288,384]{1,0:T(8,128)S(1)}, u32[]{:S(2)}) %copy-start.3) | copy-done | bytes 442392
  63.3 0.6 slice_reduce_fusion
  64.6 1.9 %subtract_bitcast_fusion = f32[1,288,384]{2,1,0:T(8,128)} fusion(f32[288,384]{1,0:T(8,128)} %copy-done.3, f32[288]{0:T(512)S(1)} %multiply_reduce_fusion), kind=kLoop, calls=%fused_computation | loop fusion | flops 110592 | bytes 885888 | tf_op jit(solution)/shard_map/broadcast_in_dim | solution.py:255
  66.5 0.8 %copy.9 = f32[1,288,384]{2,1,0:T(8,128)} copy(f32[1,288,384]{2,1,0:T(8,128)S(1)} %bitcast.4) | data formatting | bytes 884736
  (1 shorter events, 0.0 us)
Async XLA Ops:
  0.6 3.2 %copy-start.2 = (s32[288,1152]{1,0:T(8,128)S(1)}, s32[288,1152]{1,0:T(8,128)}, u32[]{:S(2)}) copy-start(s32[288,1152]{1,0:T(8,128)} %loops.1) | copy-start | bytes 3981316
  0.6 3.2 %copy-start = (f32[1,72,6144]{2,1,0:T(8,128)S(1)}, f32[1,72,6144]{2,1,0:T(8,128)}, u32[]{:S(2)}) copy-start(f32[1,72,6144]{2,1,0:T(8,128)} %phase.1) | copy-start | bytes 5308420
  3.9 1.5 %copy-start.1 = (s32[1,72,6144]{2,1,0:T(8,128)S(1)}, s32[1,72,6144]{2,1,0:T(8,128)}, u32[]{:S(2)}) copy-start(s32[1,72,6144]{2,1,0:T(8,128)} %counts.1) | copy-start | bytes 5308420
  62.5 0.8 %copy-start.3 = (f32[288,384]{1,0:T(8,128)}, f32[288,384]{1,0:T(8,128)S(1)}, u32[]{:S(2)}) copy-start(f32[288,384]{1,0:T(8,128)S(1)} %get-tuple-element.7) | copy-start | bytes 1327108

commit v2 on v1

--- a/solution.py
+++ b/solution.py
@@ -49,7 +49,7 @@
     return out
 
 
-def kernel(n, slabs, widths, doublings, phase, counts, loops, design, closure_out, shifts_out, total_out,
+def kernel(n, slabs, widths, doublings, phase, counts, loops, design_t, closure_out, shifts_out, misfit_out,
            phase_v, counts_v, sent, *rest):
     chunk_count = len(widths)
     got, rest = rest[:chunk_count], rest[chunk_count:]
@@ -58,7 +58,7 @@
     me = lax.axis_index("ifg")
     slab = lax.axis_index("slab")
     rows = phase.shape[1]
-    dates = design.shape[1]
+    dates, ifgs = design_t.shape
     columns = sum(widths)
     starts = [sum(widths[:c]) for c in range(chunk_count)]
 
@@ -67,7 +67,7 @@
         pltpu.make_async_copy(counts.at[0], counts_v, in_sem.at[1]),
     ]
     tables = [
-        pltpu.make_async_copy(design, design_v, table_sem.at[0]),
+        pltpu.make_async_copy(design_t, design_v, table_sem.at[0]),
         pltpu.make_async_copy(loops, loops_v, table_sem.at[1]),
     ]
     for copy in loads:
@@ -93,7 +93,7 @@
     for c in range(chunk_count):
         @pl.loop(0, n - 1)
         def _(step):
-            to = partner(me, n - 1 - step, n)
+            to = partner(me, n - 1 - step // 2 - (step % 2) * (n // 2), n)
             pltpu.make_async_remote_copy(
                 src_ref=sent.at[:, pl.ds(pl.multiple_of(to * columns + starts[c], 128), widths[c])],
                 dst_ref=got[c].at[me],
@@ -120,10 +120,8 @@
         copy.wait()
     loop_count = loops.shape[0]
     left[0:loop_count, :] = loops_v[...].astype(f32).astype(bf16)
-    design_b[...] = design_v[...].astype(f32).astype(bf16)
-    left[loop_count:, :] = lax.dot_general(
-        eye.astype(bf16), design_b[...], (((1,), (1,)), ((), ())), preferred_element_type=f32
-    ).astype(bf16)
+    left[loop_count:, :] = design_v[...].astype(f32).astype(bf16)
+    design_b[...] = jnp.transpose(design_v[...].astype(f32)).astype(bf16)
     matrix = dot(left[loop_count:, :], design_b[...]) + ridge_weight * eye
     normal[...] = matrix
     bound = jnp.max(jnp.sum(jnp.abs(matrix), axis=1, keepdims=True), axis=0, keepdims=True)
@@ -195,8 +193,12 @@
     everyone = rows_in.at[pl.ds(0, n * slabs - 1)]
     pltpu.make_async_copy(everyone, everyone, row_recv).wait()
     pltpu.make_async_copy(everyone, everyone, row_send).wait()
-    total_out[:, 0:padded] = jnp.sum(rows_in[:, :, 0:padded], axis=0)
-    total_out[:, padded:] = jnp.sum(rows_in[pl.ds(slab * n, n), :, padded:], axis=0)
+    date_total = jnp.sum(rows_in[:, :, 0:dates], axis=0)
+    frame_mean = jnp.sum(jnp.where(eye_bool, date_total, 0.0), axis=1, keepdims=True) * (1.0 / (slabs * n * columns))
+    shifts_out[...] = shifts_out[...] - frame_mean
+    slab_squares = jnp.sum(rows_in[pl.ds(slab * n, n), :, padded:], axis=0)
+    slab_square = jnp.sum(slab_squares, axis=1, keepdims=True)
+    misfit_out[...] = jnp.sqrt(slab_square * (1.0 / (ifgs * n * columns)) + epsilon)
 
 
 def local(phase, corrections, closure_loops, design):
@@ -212,16 +214,16 @@
     while 2 ** doublings < 4 * ifgs:
         doublings += 1
     vmem = pl.BlockSpec(memory_space=pltpu.VMEM)
-    anywhere = pl.BlockSpec(memory_space=pl.ANY)
+    in_hbm = pl.BlockSpec(memory_space=pltpu.HBM)
     dma = pltpu.SemaphoreType.DMA
-    closure, shifts, total = pl.pallas_call(
+    closure, displacement, misfit = pl.pallas_call(
         functools.partial(kernel, n, slabs, widths, doublings),
         out_shape=(
             jax.ShapeDtypeStruct((loop_count, columns), f32),
             jax.ShapeDtypeStruct((dates, columns), f32),
-            jax.ShapeDtypeStruct((1, padded + 128), f32),
+            jax.ShapeDtypeStruct((1, 1), f32),
         ),
-        in_specs=[anywhere] * 4,
+        in_specs=[in_hbm] * 4,
         out_specs=(vmem, vmem, vmem),
         scratch_shapes=[
             pltpu.VMEM((rows, pixels), f32),
@@ -229,7 +231,7 @@
             pltpu.VMEM((rows, pixels), f32),
             *[pltpu.VMEM((n, rows, width), f32) for width in widths],
             pltpu.VMEM((loop_count, ifgs), jnp.int32),
-            pltpu.VMEM((ifgs, dates), jnp.int32),
+            pltpu.VMEM((dates, ifgs), jnp.int32),
             pltpu.VMEM((ifgs, dates), bf16),
             pltpu.VMEM((loop_count + dates, ifgs), bf16),
             pltpu.VMEM((2 * dates, dates), f32),
@@ -246,12 +248,9 @@
             dma,
         ],
         compiler_params=pltpu.CompilerParams(
-            collective_id=0, has_side_effects=True, vmem_limit_bytes=48 * 1024 * 1024
+            collective_id=0, has_side_effects=True, vmem_limit_bytes=65_500_000
         ),
-    )(phase, corrections, closure_loops, design)
-    frame_mean = total[0, 0:dates] / (slabs * pixels)
-    displacement = shifts - frame_mean[:, None]
-    misfit = jnp.sqrt(jnp.sum(total[0, padded:]) / (ifgs * pixels) + epsilon)
+    )(phase, corrections, closure_loops, design.T)
     return (closure[None], displacement[None], misfit.reshape(1))
 
 

time: 68.6 us -> 63.3 us (0.923)
  local copies, waits for them, and re-layouts: 6.23 us -> 3.61 us
  other arithmetic: 2.5 us -> 0 us
    unnamed x10 -> x2, local copies, waits for them, and re-layouts: 6.23 us -> 3.61 us
    broadcast_in_dim x1 -> x0, other arithmetic: 1.88 us -> none  [local(): return (closure[None], displacement[None], misfit.reshape(1))]
where the time goes in v2:
time: 63.3 us; the launch traced here: 63.1 us
  Pallas kernels  57 us (90%)
  local copies, waits for them, and re-layouts  3.61 us (6%)
  between operations  2.44 us (4%)
    pallas_call x1, Pallas kernels, local(): pl.pallas_call(functools.partial(kernel, n, slabs, widths, doublings), ou...  57 us
    unnamed x2, local copies, waits for them, and re-layouts  3.61 us

profile of v2, /device:TPU:0, one launch (start us, length us, event | category | flops | bytes accessed | tf_op | source)
XLA Modules:
  0.0 63.1 jit_solution(13716790225110520920)
XLA Ops:
  0.6 57.0 %shard_map.67 = (f32[288,384]{1,0:T(8,128)}, f32[288,384]{1,0:T(8,128)}, f32[1,1]{1,0:T(1,128)}) custom-call(f32[1,72,6144]{2,1,0:T(8,128)} %phase.1, s32[1,72,6144]{2,1,0:T(8,128)} %counts.1, s32[288,1152]{1,0:T(8,128)} %loops.1, s32[288,1152]{1,0:T(8,128)} %bitcast.4), custom_call_target="tpu_custom_call" | custom-call | tf_op jit(solution)/shard_map/pallas_call | solution.py:219
  57.7 1.8 %copy.10 = f32[1,288,384]{2,1,0:T(8,128)} copy(f32[1,288,384]{2,1,0:T(8,128)} %bitcast.6) | data formatting | bytes 884736
  59.5 1.8 %copy.11 = f32[1,288,384]{2,1,0:T(8,128)} copy(f32[1,288,384]{2,1,0:T(8,128)} %bitcast.5) | data formatting | bytes 884736

commit v3 on v2

--- a/solution.py
+++ b/solution.py
@@ -219,8 +219,8 @@
     closure, displacement, misfit = pl.pallas_call(
         functools.partial(kernel, n, slabs, widths, doublings),
         out_shape=(
-            jax.ShapeDtypeStruct((loop_count, columns), f32),
-            jax.ShapeDtypeStruct((dates, columns), f32),
+            pltpu.VMEM((loop_count, columns), f32),
+            pltpu.VMEM((dates, columns), f32),
             jax.ShapeDtypeStruct((1, 1), f32),
         ),
         in_specs=[in_hbm] * 4,
@@ -248,7 +248,7 @@
             dma,
         ],
         compiler_params=pltpu.CompilerParams(
-            collective_id=0, has_side_effects=True, vmem_limit_bytes=65_500_000
+            collective_id=0, has_side_effects=True, vmem_limit_bytes=62_000_000
         ),
     )(phase, corrections, closure_loops, design.T)
     return (closure[None], displacement[None], misfit.reshape(1))

time: 63.3 us -> 60.7 us (0.959)
  local copies, waits for them, and re-layouts: 3.61 us -> 1.53 us
    unnamed x2, local copies, waits for them, and re-layouts: 3.61 us -> 1.53 us
where the time goes in v3:
time: 60.7 us; the launch traced here: 60.5 us
  Pallas kernels  56.7 us (93%)
  between operations  2.33 us (4%)
  local copies, waits for them, and re-layouts  1.53 us (3%)
    pallas_call x1, Pallas kernels, local(): pl.pallas_call(functools.partial(kernel, n, slabs, widths, doublings), ou...  56.7 us
    unnamed x2, local copies, waits for them, and re-layouts  1.53 us

profile of v3, /device:TPU:0, one launch (start us, length us, event | category | flops | bytes accessed | tf_op | source)
XLA Modules:
  0.0 60.5 jit_solution(4709354154651430573)
XLA Ops:
  0.6 56.7 %shard_map.67 = (f32[288,384]{1,0:T(8,128)S(1)}, f32[288,384]{1,0:T(8,128)S(1)}, f32[1,1]{1,0:T(1,128)}) custom-call(f32[1,72,6144]{2,1,0:T(8,128)} %phase.1, s32[1,72,6144]{2,1,0:T(8,128)} %counts.1, s32[288,1152]{1,0:T(8,128)} %loops.1, s32[288,1152]{1,0:T(8,128)} %bitcast.6), custom_call_target="tpu_custom_call" | custom-call | tf_op jit(solution)/shard_map/pallas_call | solution.py:219
  57.3 0.8 %copy.10 = f32[1,288,384]{2,1,0:T(8,128)} copy(f32[1,288,384]{2,1,0:T(8,128)S(1)} %bitcast.5) | data formatting | bytes 884736
  58.1 0.8 %copy.11 = f32[1,288,384]{2,1,0:T(8,128)} copy(f32[1,288,384]{2,1,0:T(8,128)S(1)} %bitcast.4) | data formatting | bytes 884736
